TPU v7x, 32 devices: a whole 2x2x4 slice. The times are simulated.
32 devices in a mesh: blk: 8 (over y, x, core), grp: 4 (over z).
Axes of the slice: x: 2, y: 2, z: 4, core: 2. Of those that a mesh axis runs over, the one named last changes fastest.
Arguments:
- image_embeds: bfloat16 [4096, 1152], P(('blk', 'grp')), may hold values from -6 to 6
- text_embeds: bfloat16 [4096, 1152], P(('blk', 'grp')), may hold values from -6 to 6
Outputs:
- image_embed_gradient: bfloat16 [4096, 1152], P(('blk', 'grp'))
- text_embed_gradient: bfloat16 [4096, 1152], P(('blk', 'grp'))
All inputs are finite; a program needn't handle non-finite values.
Results may differ from a plain program's by a relative error of at most 0.0059.
Values may be sent and summed in bfloat16 or wider, within the bound.
A program may use at most 64 MiB of HBM per device.

v0:
```python
import jax
import jax.numpy as jnp
from jax import lax
from jax.sharding import PartitionSpec as P

LOGIT_SCALE = 10.0
BIAS_LOGIT = -2.0
EPSILON = 1e-06


def shifted(value, axis, steps):
    count = lax.axis_size(axis)
    pairs = [(source, (source + steps) % count) for source in range(count)]
    return lax.ppermute(value, axis, pairs)


def normalize(values):
    wide = values.astype(jnp.float32)
    length = jnp.sqrt(jnp.sum(wide * wide, axis=-1, keepdims=True) + EPSILON)
    return (wide / length, length)


def undo_normalization(grad, unit, length):
    inner = jnp.sum(unit * grad, axis=-1, keepdims=True)
    return (grad - unit * inner) / length


def pair_weights(image_block, text_block, is_first):
    pair_logits = (
        LOGIT_SCALE
        * lax.dot_general(
            image_block, text_block, (((1,), (1,)), ((), ())), preferred_element_type=jnp.float32
        )
        + BIAS_LOGIT
    )
    count = pair_logits.shape[-1]
    diagonal_mask = jnp.eye(count, dtype=bool) & is_first
    weights = jnp.where(diagonal_mask, -jax.nn.sigmoid(-pair_logits), jax.nn.sigmoid(pair_logits))
    return weights.astype(jnp.bfloat16)


def text_terms(weights, image_block):
    return lax.dot_general(
        weights, image_block, (((0,), (0,)), ((), ())), preferred_element_type=jnp.float32
    )


def per_device(image_embeds, text_embeds):
    cycle_size = lax.axis_size(("blk", "grp"))
    window = min(20, cycle_size // 2)
    image_normalized, image_norm = normalize(image_embeds)
    text_normalized, text_norm = normalize(text_embeds)
    image_reduced = image_normalized.astype(jnp.bfloat16)
    text_low = text_normalized.astype(jnp.bfloat16)

    def advance(running, offset):
        text_block, image_block, text_total, image_total = running
        is_first = offset == 0
        weights = pair_weights(image_reduced, text_block, is_first)
        image_total = image_total + jnp.dot(weights, text_block, preferred_element_type=jnp.float32)
        passed = shifted(text_block, ("blk", "grp"), 1)
        own_weights = pair_weights(image_block, text_low, is_first)
        text_total = text_total + text_terms(own_weights, image_block)
        image_block = shifted(image_block, ("blk", "grp"), -1)
        return ((passed, image_block, text_total, image_total), weights)

    zeros = jnp.zeros(image_reduced.shape, jnp.float32)
    (text_block, image_block, text_total, image_total), stored = lax.scan(
        advance, (text_low, image_reduced, zeros, zeros), jnp.arange(window - 1, dtype=jnp.int32)
    )
    last_first = jnp.asarray(window - 1) == 0
    final_weights = pair_weights(image_reduced, text_block, last_first)
    image_total = image_total + jnp.dot(
        final_weights, text_block, preferred_element_type=jnp.float32
    )
    own_weights = pair_weights(image_block, text_low, last_first)
    text_total = text_total + text_terms(own_weights, image_block)
    image_embed_gradient = undo_normalization(
        LOGIT_SCALE * image_total, image_normalized, image_norm
    ).astype(jnp.bfloat16)
    text_embed_gradient = undo_normalization(
        LOGIT_SCALE * text_total, text_normalized, text_norm
    ).astype(jnp.bfloat16)
    return (image_embed_gradient, text_embed_gradient)


def solution(mesh):
    placed = (P(("blk", "grp"), None), P(("blk", "grp"), None))
    return jax.shard_map(
        per_device,
        mesh=mesh,
        in_specs=placed,
        out_specs=(P(("blk", "grp"), None), P(("blk", "grp"), None)),
        check_vma=False,
    )
```

profile of v0, /device:TPU:0, one launch (start us, length us, event | category | flops | bytes accessed | tf_op | source)
XLA Modules:
  0.0 249.4 jit_solution(9734338038036327102)
XLA Ops:
  2.3 243.9 %while.17 = (s32[]{:T(128)}, bf16[128,1152]{1,0:T(8,128)(2,1)S(1)}, bf16[128,1152]{1,0:T(8,128)(2,1)S(1)}, f32[128,1152]{1,0:T(8,128)S(1)}, f32[128,1152]{1,0:T(...) while((s32[]{:T(128)}, bf16[128,1152]{1,0:T(8,128)(2,1)S(1)}, ...), condition=%wide.region_3.4_spmd.clone, body=%wide.region_2.3_spmd.clone.sunk | while | flops 151977984 | bytes 7078111 | solution.py:68
  2.4 3.1 %collective-permute-start = (bf16[128,1152]{1,0:T(8,128)(2,1)S(1)}, bf16[128,1152]{1,0:T(8,128)(2,1)S(1)}, u32[]{:S(2)}, u32[]{:S(2)}) collective-permute-start(bf16[128,1152]{1,0:T(8,128)(2,1)S(1)} %copy.10), channel_id=1, source_target_pairs={{0,1},{1,2},{2,3},{3,4},{4,5},{5,6},{6,7},{7,8},{8,9},{9,10},{10,1... | collective-permute-start | bytes 884744 | tf_op jit(solution)/shard_map/while/body/eval_jaxpr/ppermute | solution.py:14
  5.5 3.4 %collective-permute-start.1 = (bf16[128,1152]{1,0:T(8,128)(2,1)S(1)}, bf16[128,1152]{1,0:T(8,128)(2,1)S(1)}, u32[]{:S(2)}, u32[]{:S(2)}) collective-permute-start(bf16[128,1152]{1,0:T(8,128)(2,1)S(1)} %copy.11), channel_id=1, source_target_pairs={{0,31},{1,0},{2,1},{3,2},{4,3},{5,4},{6,5},{7,6},{8,7},{9,8},{10,9... | collective-permute-start | bytes 884744 | tf_op jit(solution)/shard_map/while/body/eval_jaxpr/ppermute | solution.py:14
  11.5 4.1 %collective-permute-done = bf16[128,1152]{1,0:T(8,128)(2,1)S(1)} collective-permute-done((bf16[128,1152]{1,0:T(8,128)(2,1)S(1)}, bf16[128,1152]{1,0:T(8,128)(2,1)S(1)}, u32[]{:S(2)}, u32[]{:S(2)}) %collective-permute-start) | collective-permute-done | bytes 294944 | tf_op jit(solution)/shard_map/while/body/eval_jaxpr/ppermute | solution.py:14
  15.6 4.7 %collective-permute-done.1 = bf16[128,1152]{1,0:T(8,128)(2,1)S(1)} collective-permute-done((bf16[128,1152]{1,0:T(8,128)(2,1)S(1)}, bf16[128,1152]{1,0:T(8,128)(2,1)S(1)}, u32[]{:S(2)}, u32[]{:S(2)}) %collective-permute-start.1) | collective-permute-done | bytes 294944 | tf_op jit(solution)/shard_map/while/body/eval_jaxpr/ppermute | solution.py:14
  20.4 1.6 collective-permute-start
  22.0 3.8 %collective-permute-start.1 = (bf16[128,1152]{1,0:T(8,128)(2,1)S(1)}, bf16[128,1152]{1,0:T(8,128)(2,1)S(1)}, u32[]{:S(2)}, u32[]{:S(2)}) collective-permute-start(bf16[128,1152]{1,0:T(8,128)(2,1)S(1)} %copy.11), channel_id=1, source_target_pairs={{0,31},{1,0},{2,1},{3,2},{4,3},{5,4},{6,5},{7,6},{8,7},{9,8},{10,9... | collective-permute-start | bytes 884744 | tf_op jit(solution)/shard_map/while/body/eval_jaxpr/ppermute | solution.py:14
  28.4 4.9 %collective-permute-done = bf16[128,1152]{1,0:T(8,128)(2,1)S(1)} collective-permute-done((bf16[128,1152]{1,0:T(8,128)(2,1)S(1)}, bf16[128,1152]{1,0:T(8,128)(2,1)S(1)}, u32[]{:S(2)}, u32[]{:S(2)}) %collective-permute-start) | collective-permute-done | bytes 294944 | tf_op jit(solution)/shard_map/while/body/eval_jaxpr/ppermute | solution.py:14
  33.4 3.4 %collective-permute-done.1 = bf16[128,1152]{1,0:T(8,128)(2,1)S(1)} collective-permute-done((bf16[128,1152]{1,0:T(8,128)(2,1)S(1)}, bf16[128,1152]{1,0:T(8,128)(2,1)S(1)}, u32[]{:S(2)}, u32[]{:S(2)}) %collective-permute-start.1) | collective-permute-done | bytes 294944 | tf_op jit(solution)/shard_map/while/body/eval_jaxpr/ppermute | solution.py:14
  37.5 4.7 %collective-permute-start.1 = (bf16[128,1152]{1,0:T(8,128)(2,1)S(1)}, bf16[128,1152]{1,0:T(8,128)(2,1)S(1)}, u32[]{:S(2)}, u32[]{:S(2)}) collective-permute-start(bf16[128,1152]{1,0:T(8,128)(2,1)S(1)} %copy.11), channel_id=1, source_target_pairs={{0,31},{1,0},{2,1},{3,2},{4,3},{5,4},{6,5},{7,6},{8,7},{9,8},{10,9... | collective-permute-start | bytes 884744 | tf_op jit(solution)/shard_map/while/body/eval_jaxpr/ppermute | solution.py:14
  44.8 4.9 %collective-permute-done = bf16[128,1152]{1,0:T(8,128)(2,1)S(1)} collective-permute-done((bf16[128,1152]{1,0:T(8,128)(2,1)S(1)}, bf16[128,1152]{1,0:T(8,128)(2,1)S(1)}, u32[]{:S(2)}, u32[]{:S(2)}) %collective-permute-start) | collective-permute-done | bytes 294944 | tf_op jit(solution)/shard_map/while/body/eval_jaxpr/ppermute | solution.py:14
  49.8 2.8 %collective-permute-done.1 = bf16[128,1152]{1,0:T(8,128)(2,1)S(1)} collective-permute-done((bf16[128,1152]{1,0:T(8,128)(2,1)S(1)}, bf16[128,1152]{1,0:T(8,128)(2,1)S(1)}, u32[]{:S(2)}, u32[]{:S(2)}) %collective-permute-start.1) | collective-permute-done | bytes 294944 | tf_op jit(solution)/shard_map/while/body/eval_jaxpr/ppermute | solution.py:14
  53.7 4.4 %collective-permute-start.1 = (bf16[128,1152]{1,0:T(8,128)(2,1)S(1)}, bf16[128,1152]{1,0:T(8,128)(2,1)S(1)}, u32[]{:S(2)}, u32[]{:S(2)}) collective-permute-start(bf16[128,1152]{1,0:T(8,128)(2,1)S(1)} %copy.11), channel_id=1, source_target_pairs={{0,31},{1,0},{2,1},{3,2},{4,3},{5,4},{6,5},{7,6},{8,7},{9,8},{10,9... | collective-permute-start | bytes 884744 | tf_op jit(solution)/shard_map/while/body/eval_jaxpr/ppermute | solution.py:14
  60.6 4.9 %collective-permute-done = bf16[128,1152]{1,0:T(8,128)(2,1)S(1)} collective-permute-done((bf16[128,1152]{1,0:T(8,128)(2,1)S(1)}, bf16[128,1152]{1,0:T(8,128)(2,1)S(1)}, u32[]{:S(2)}, u32[]{:S(2)}) %collective-permute-start) | collective-permute-done | bytes 294944 | tf_op jit(solution)/shard_map/while/body/eval_jaxpr/ppermute | solution.py:14
  65.6 3.2 %collective-permute-done.1 = bf16[128,1152]{1,0:T(8,128)(2,1)S(1)} collective-permute-done((bf16[128,1152]{1,0:T(8,128)(2,1)S(1)}, bf16[128,1152]{1,0:T(8,128)(2,1)S(1)}, u32[]{:S(2)}, u32[]{:S(2)}) %collective-permute-start.1) | collective-permute-done | bytes 294944 | tf_op jit(solution)/shard_map/while/body/eval_jaxpr/ppermute | solution.py:14
  69.8 4.5 %collective-permute-start.1 = (bf16[128,1152]{1,0:T(8,128)(2,1)S(1)}, bf16[128,1152]{1,0:T(8,128)(2,1)S(1)}, u32[]{:S(2)}, u32[]{:S(2)}) collective-permute-start(bf16[128,1152]{1,0:T(8,128)(2,1)S(1)} %copy.11), channel_id=1, source_target_pairs={{0,31},{1,0},{2,1},{3,2},{4,3},{5,4},{6,5},{7,6},{8,7},{9,8},{10,9... | collective-permute-start | bytes 884744 | tf_op jit(solution)/shard_map/while/body/eval_jaxpr/ppermute | solution.py:14
  76.9 4.9 %collective-permute-done = bf16[128,1152]{1,0:T(8,128)(2,1)S(1)} collective-permute-done((bf16[128,1152]{1,0:T(8,128)(2,1)S(1)}, bf16[128,1152]{1,0:T(8,128)(2,1)S(1)}, u32[]{:S(2)}, u32[]{:S(2)}) %collective-permute-start) | collective-permute-done | bytes 294944 | tf_op jit(solution)/shard_map/while/body/eval_jaxpr/ppermute | solution.py:14
  81.8 3.1 %collective-permute-done.1 = bf16[128,1152]{1,0:T(8,128)(2,1)S(1)} collective-permute-done((bf16[128,1152]{1,0:T(8,128)(2,1)S(1)}, bf16[128,1152]{1,0:T(8,128)(2,1)S(1)}, u32[]{:S(2)}, u32[]{:S(2)}) %collective-permute-start.1) | collective-permute-done | bytes 294944 | tf_op jit(solution)/shard_map/while/body/eval_jaxpr/ppermute | solution.py:14
  86.3 4.1 %collective-permute-start.1 = (bf16[128,1152]{1,0:T(8,128)(2,1)S(1)}, bf16[128,1152]{1,0:T(8,128)(2,1)S(1)}, u32[]{:S(2)}, u32[]{:S(2)}) collective-permute-start(bf16[128,1152]{1,0:T(8,128)(2,1)S(1)} %copy.11), channel_id=1, source_target_pairs={{0,31},{1,0},{2,1},{3,2},{4,3},{5,4},{6,5},{7,6},{8,7},{9,8},{10,9... | collective-permute-start | bytes 884744 | tf_op jit(solution)/shard_map/while/body/eval_jaxpr/ppermute | solution.py:14
  93.0 5.0 %collective-permute-done = bf16[128,1152]{1,0:T(8,128)(2,1)S(1)} collective-permute-done((bf16[128,1152]{1,0:T(8,128)(2,1)S(1)}, bf16[128,1152]{1,0:T(8,128)(2,1)S(1)}, u32[]{:S(2)}, u32[]{:S(2)}) %collective-permute-start) | collective-permute-done | bytes 294944 | tf_op jit(solution)/shard_map/while/body/eval_jaxpr/ppermute | solution.py:14
  97.9 2.8 %collective-permute-done.1 = bf16[128,1152]{1,0:T(8,128)(2,1)S(1)} collective-permute-done((bf16[128,1152]{1,0:T(8,128)(2,1)S(1)}, bf16[128,1152]{1,0:T(8,128)(2,1)S(1)}, u32[]{:S(2)}, u32[]{:S(2)}) %collective-permute-start.1) | collective-permute-done | bytes 294944 | tf_op jit(solution)/shard_map/while/body/eval_jaxpr/ppermute | solution.py:14
  102.1 4.1 %collective-permute-start.1 = (bf16[128,1152]{1,0:T(8,128)(2,1)S(1)}, bf16[128,1152]{1,0:T(8,128)(2,1)S(1)}, u32[]{:S(2)}, u32[]{:S(2)}) collective-permute-start(bf16[128,1152]{1,0:T(8,128)(2,1)S(1)} %copy.11), channel_id=1, source_target_pairs={{0,31},{1,0},{2,1},{3,2},{4,3},{5,4},{6,5},{7,6},{8,7},{9,8},{10,9... | collective-permute-start | bytes 884744 | tf_op jit(solution)/shard_map/while/body/eval_jaxpr/ppermute | solution.py:14
  108.8 4.8 %collective-permute-done = bf16[128,1152]{1,0:T(8,128)(2,1)S(1)} collective-permute-done((bf16[128,1152]{1,0:T(8,128)(2,1)S(1)}, bf16[128,1152]{1,0:T(8,128)(2,1)S(1)}, u32[]{:S(2)}, u32[]{:S(2)}) %collective-permute-start) | collective-permute-done | bytes 294944 | tf_op jit(solution)/shard_map/while/body/eval_jaxpr/ppermute | solution.py:14
  113.6 3.6 %collective-permute-done.1 = bf16[128,1152]{1,0:T(8,128)(2,1)S(1)} collective-permute-done((bf16[128,1152]{1,0:T(8,128)(2,1)S(1)}, bf16[128,1152]{1,0:T(8,128)(2,1)S(1)}, u32[]{:S(2)}, u32[]{:S(2)}) %collective-permute-start.1) | collective-permute-done | bytes 294944 | tf_op jit(solution)/shard_map/while/body/eval_jaxpr/ppermute | solution.py:14
  118.2 4.5 %collective-permute-start.1 = (bf16[128,1152]{1,0:T(8,128)(2,1)S(1)}, bf16[128,1152]{1,0:T(8,128)(2,1)S(1)}, u32[]{:S(2)}, u32[]{:S(2)}) collective-permute-start(bf16[128,1152]{1,0:T(8,128)(2,1)S(1)} %copy.11), channel_id=1, source_target_pairs={{0,31},{1,0},{2,1},{3,2},{4,3},{5,4},{6,5},{7,6},{8,7},{9,8},{10,9... | collective-permute-start | bytes 884744 | tf_op jit(solution)/shard_map/while/body/eval_jaxpr/ppermute | solution.py:14
  125.3 4.9 %collective-permute-done = bf16[128,1152]{1,0:T(8,128)(2,1)S(1)} collective-permute-done((bf16[128,1152]{1,0:T(8,128)(2,1)S(1)}, bf16[128,1152]{1,0:T(8,128)(2,1)S(1)}, u32[]{:S(2)}, u32[]{:S(2)}) %collective-permute-start) | collective-permute-done | bytes 294944 | tf_op jit(solution)/shard_map/while/body/eval_jaxpr/ppermute | solution.py:14
  130.3 2.9 %collective-permute-done.1 = bf16[128,1152]{1,0:T(8,128)(2,1)S(1)} collective-permute-done((bf16[128,1152]{1,0:T(8,128)(2,1)S(1)}, bf16[128,1152]{1,0:T(8,128)(2,1)S(1)}, u32[]{:S(2)}, u32[]{:S(2)}) %collective-permute-start.1) | collective-permute-done | bytes 294944 | tf_op jit(solution)/shard_map/while/body/eval_jaxpr/ppermute | solution.py:14
  134.6 4.1 %collective-permute-start.1 = (bf16[128,1152]{1,0:T(8,128)(2,1)S(1)}, bf16[128,1152]{1,0:T(8,128)(2,1)S(1)}, u32[]{:S(2)}, u32[]{:S(2)}) collective-permute-start(bf16[128,1152]{1,0:T(8,128)(2,1)S(1)} %copy.11), channel_id=1, source_target_pairs={{0,31},{1,0},{2,1},{3,2},{4,3},{5,4},{6,5},{7,6},{8,7},{9,8},{10,9... | collective-permute-start | bytes 884744 | tf_op jit(solution)/shard_map/while/body/eval_jaxpr/ppermute | solution.py:14
  141.2 4.9 %collective-permute-done = bf16[128,1152]{1,0:T(8,128)(2,1)S(1)} collective-permute-done((bf16[128,1152]{1,0:T(8,128)(2,1)S(1)}, bf16[128,1152]{1,0:T(8,128)(2,1)S(1)}, u32[]{:S(2)}, u32[]{:S(2)}) %collective-permute-start) | collective-permute-done | bytes 294944 | tf_op jit(solution)/shard_map/while/body/eval_jaxpr/ppermute | solution.py:14
  146.2 3.4 %collective-permute-done.1 = bf16[128,1152]{1,0:T(8,128)(2,1)S(1)} collective-permute-done((bf16[128,1152]{1,0:T(8,128)(2,1)S(1)}, bf16[128,1152]{1,0:T(8,128)(2,1)S(1)}, u32[]{:S(2)}, u32[]{:S(2)}) %collective-permute-start.1) | collective-permute-done | bytes 294944 | tf_op jit(solution)/shard_map/while/body/eval_jaxpr/ppermute | solution.py:14
  150.3 4.8 %collective-permute-start.1 = (bf16[128,1152]{1,0:T(8,128)(2,1)S(1)}, bf16[128,1152]{1,0:T(8,128)(2,1)S(1)}, u32[]{:S(2)}, u32[]{:S(2)}) collective-permute-start(bf16[128,1152]{1,0:T(8,128)(2,1)S(1)} %copy.11), channel_id=1, source_target_pairs={{0,31},{1,0},{2,1},{3,2},{4,3},{5,4},{6,5},{7,6},{8,7},{9,8},{10,9... | collective-permute-start | bytes 884744 | tf_op jit(solution)/shard_map/while/body/eval_jaxpr/ppermute | solution.py:14
  157.7 4.9 %collective-permute-done = bf16[128,1152]{1,0:T(8,128)(2,1)S(1)} collective-permute-done((bf16[128,1152]{1,0:T(8,128)(2,1)S(1)}, bf16[128,1152]{1,0:T(8,128)(2,1)S(1)}, u32[]{:S(2)}, u32[]{:S(2)}) %collective-permute-start) | collective-permute-done | bytes 294944 | tf_op jit(solution)/shard_map/while/body/eval_jaxpr/ppermute | solution.py:14
  162.6 2.8 %collective-permute-done.1 = bf16[128,1152]{1,0:T(8,128)(2,1)S(1)} collective-permute-done((bf16[128,1152]{1,0:T(8,128)(2,1)S(1)}, bf16[128,1152]{1,0:T(8,128)(2,1)S(1)}, u32[]{:S(2)}, u32[]{:S(2)}) %collective-permute-start.1) | collective-permute-done | bytes 294944 | tf_op jit(solution)/shard_map/while/body/eval_jaxpr/ppermute | solution.py:14
  166.7 4.3 %collective-permute-start.1 = (bf16[128,1152]{1,0:T(8,128)(2,1)S(1)}, bf16[128,1152]{1,0:T(8,128)(2,1)S(1)}, u32[]{:S(2)}, u32[]{:S(2)}) collective-permute-start(bf16[128,1152]{1,0:T(8,128)(2,1)S(1)} %copy.11), channel_id=1, source_target_pairs={{0,31},{1,0},{2,1},{3,2},{4,3},{5,4},{6,5},{7,6},{8,7},{9,8},{10,9... | collective-permute-start | bytes 884744 | tf_op jit(solution)/shard_map/while/body/eval_jaxpr/ppermute | solution.py:14
  173.5 4.9 %collective-permute-done = bf16[128,1152]{1,0:T(8,128)(2,1)S(1)} collective-permute-done((bf16[128,1152]{1,0:T(8,128)(2,1)S(1)}, bf16[128,1152]{1,0:T(8,128)(2,1)S(1)}, u32[]{:S(2)}, u32[]{:S(2)}) %collective-permute-start) | collective-permute-done | bytes 294944 | tf_op jit(solution)/shard_map/while/body/eval_jaxpr/ppermute | solution.py:14
  178.4 3.3 %collective-permute-done.1 = bf16[128,1152]{1,0:T(8,128)(2,1)S(1)} collective-permute-done((bf16[128,1152]{1,0:T(8,128)(2,1)S(1)}, bf16[128,1152]{1,0:T(8,128)(2,1)S(1)}, u32[]{:S(2)}, u32[]{:S(2)}) %collective-permute-start.1) | collective-permute-done | bytes 294944 | tf_op jit(solution)/shard_map/while/body/eval_jaxpr/ppermute | solution.py:14
  182.8 4.5 %collective-permute-start.1 = (bf16[128,1152]{1,0:T(8,128)(2,1)S(1)}, bf16[128,1152]{1,0:T(8,128)(2,1)S(1)}, u32[]{:S(2)}, u32[]{:S(2)}) collective-permute-start(bf16[128,1152]{1,0:T(8,128)(2,1)S(1)} %copy.11), channel_id=1, source_target_pairs={{0,31},{1,0},{2,1},{3,2},{4,3},{5,4},{6,5},{7,6},{8,7},{9,8},{10,9... | collective-permute-start | bytes 884744 | tf_op jit(solution)/shard_map/while/body/eval_jaxpr/ppermute | solution.py:14
  189.9 4.9 %collective-permute-done = bf16[128,1152]{1,0:T(8,128)(2,1)S(1)} collective-permute-done((bf16[128,1152]{1,0:T(8,128)(2,1)S(1)}, bf16[128,1152]{1,0:T(8,128)(2,1)S(1)}, u32[]{:S(2)}, u32[]{:S(2)}) %collective-permute-start) | collective-permute-done | bytes 294944 | tf_op jit(solution)/shard_map/while/body/eval_jaxpr/ppermute | solution.py:14
  194.8 3.0 %collective-permute-done.1 = bf16[128,1152]{1,0:T(8,128)(2,1)S(1)} collective-permute-done((bf16[128,1152]{1,0:T(8,128)(2,1)S(1)}, bf16[128,1152]{1,0:T(8,128)(2,1)S(1)}, u32[]{:S(2)}, u32[]{:S(2)}) %collective-permute-start.1) | collective-permute-done | bytes 294944 | tf_op jit(solution)/shard_map/while/body/eval_jaxpr/ppermute | solution.py:14
  198.9 4.3 %collective-permute-start.1 = (bf16[128,1152]{1,0:T(8,128)(2,1)S(1)}, bf16[128,1152]{1,0:T(8,128)(2,1)S(1)}, u32[]{:S(2)}, u32[]{:S(2)}) collective-permute-start(bf16[128,1152]{1,0:T(8,128)(2,1)S(1)} %copy.11), channel_id=1, source_target_pairs={{0,31},{1,0},{2,1},{3,2},{4,3},{5,4},{6,5},{7,6},{8,7},{9,8},{10,9... | collective-permute-start | bytes 884744 | tf_op jit(solution)/shard_map/while/body/eval_jaxpr/ppermute | solution.py:14
  205.9 4.9 %collective-permute-done = bf16[128,1152]{1,0:T(8,128)(2,1)S(1)} collective-permute-done((bf16[128,1152]{1,0:T(8,128)(2,1)S(1)}, bf16[128,1152]{1,0:T(8,128)(2,1)S(1)}, u32[]{:S(2)}, u32[]{:S(2)}) %collective-permute-start) | collective-permute-done | bytes 294944 | tf_op jit(solution)/shard_map/while/body/eval_jaxpr/ppermute | solution.py:14
  210.8 2.8 %collective-permute-done.1 = bf16[128,1152]{1,0:T(8,128)(2,1)S(1)} collective-permute-done((bf16[128,1152]{1,0:T(8,128)(2,1)S(1)}, bf16[128,1152]{1,0:T(8,128)(2,1)S(1)}, u32[]{:S(2)}, u32[]{:S(2)}) %collective-permute-start.1) | collective-permute-done | bytes 294944 | tf_op jit(solution)/shard_map/while/body/eval_jaxpr/ppermute | solution.py:14
  215.0 4.0 %collective-permute-start.1 = (bf16[128,1152]{1,0:T(8,128)(2,1)S(1)}, bf16[128,1152]{1,0:T(8,128)(2,1)S(1)}, u32[]{:S(2)}, u32[]{:S(2)}) collective-permute-start(bf16[128,1152]{1,0:T(8,128)(2,1)S(1)} %copy.11), channel_id=1, source_target_pairs={{0,31},{1,0},{2,1},{3,2},{4,3},{5,4},{6,5},{7,6},{8,7},{9,8},{10,9... | collective-permute-start | bytes 884744 | tf_op jit(solution)/shard_map/while/body/eval_jaxpr/ppermute | solution.py:14
  221.7 4.9 %collective-permute-done = bf16[128,1152]{1,0:T(8,128)(2,1)S(1)} collective-permute-done((bf16[128,1152]{1,0:T(8,128)(2,1)S(1)}, bf16[128,1152]{1,0:T(8,128)(2,1)S(1)}, u32[]{:S(2)}, u32[]{:S(2)}) %collective-permute-start) | collective-permute-done | bytes 294944 | tf_op jit(solution)/shard_map/while/body/eval_jaxpr/ppermute | solution.py:14
  226.6 3.5 %collective-permute-done.1 = bf16[128,1152]{1,0:T(8,128)(2,1)S(1)} collective-permute-done((bf16[128,1152]{1,0:T(8,128)(2,1)S(1)}, bf16[128,1152]{1,0:T(8,128)(2,1)S(1)}, u32[]{:S(2)}, u32[]{:S(2)}) %collective-permute-start.1) | collective-permute-done | bytes 294944 | tf_op jit(solution)/shard_map/while/body/eval_jaxpr/ppermute | solution.py:14
  231.2 4.5 %collective-permute-start.1 = (bf16[128,1152]{1,0:T(8,128)(2,1)S(1)}, bf16[128,1152]{1,0:T(8,128)(2,1)S(1)}, u32[]{:S(2)}, u32[]{:S(2)}) collective-permute-start(bf16[128,1152]{1,0:T(8,128)(2,1)S(1)} %copy.11), channel_id=1, source_target_pairs={{0,31},{1,0},{2,1},{3,2},{4,3},{5,4},{6,5},{7,6},{8,7},{9,8},{10,9... | collective-permute-start | bytes 884744 | tf_op jit(solution)/shard_map/while/body/eval_jaxpr/ppermute | solution.py:14
  238.2 4.9 %collective-permute-done = bf16[128,1152]{1,0:T(8,128)(2,1)S(1)} collective-permute-done((bf16[128,1152]{1,0:T(8,128)(2,1)S(1)}, bf16[128,1152]{1,0:T(8,128)(2,1)S(1)}, u32[]{:S(2)}, u32[]{:S(2)}) %collective-permute-start) | collective-permute-done | bytes 294944 | tf_op jit(solution)/shard_map/while/body/eval_jaxpr/ppermute | solution.py:14
  243.1 3.1 %collective-permute-done.1 = bf16[128,1152]{1,0:T(8,128)(2,1)S(1)} collective-permute-done((bf16[128,1152]{1,0:T(8,128)(2,1)S(1)}, bf16[128,1152]{1,0:T(8,128)(2,1)S(1)}, u32[]{:S(2)}, u32[]{:S(2)}) %collective-permute-start.1) | collective-permute-done | bytes 294944 | tf_op jit(solution)/shard_map/while/body/eval_jaxpr/ppermute | solution.py:14
  (106 shorter events, 48.2 us)
Async XLA Ops:
  0.6 1.2 copy-start.1
  0.6 1.4 copy-start
  2.4 13.3 %collective-permute-start = (bf16[128,1152]{1,0:T(8,128)(2,1)S(1)}, bf16[128,1152]{1,0:T(8,128)(2,1)S(1)}, u32[]{:S(2)}, u32[]{:S(2)}) collective-permute-start(bf16[128,1152]{1,0:T(8,128)(2,1)S(1)} %copy.10), channel_id=1, source_target_pairs={{0,1},{1,2},{2,3},{3,4},{4,5},{5,6},{6,7},{7,8},{8,9},{9,10},{10,1... | collective-permute-start | bytes 884744 | tf_op jit(solution)/shard_map/while/body/eval_jaxpr/ppermute | solution.py:14
  5.5 14.8 %collective-permute-start.1 = (bf16[128,1152]{1,0:T(8,128)(2,1)S(1)}, bf16[128,1152]{1,0:T(8,128)(2,1)S(1)}, u32[]{:S(2)}, u32[]{:S(2)}) collective-permute-start(bf16[128,1152]{1,0:T(8,128)(2,1)S(1)} %copy.11), channel_id=1, source_target_pairs={{0,31},{1,0},{2,1},{3,2},{4,3},{5,4},{6,5},{7,6},{8,7},{9,8},{10,9... | collective-permute-start | bytes 884744 | tf_op jit(solution)/shard_map/while/body/eval_jaxpr/ppermute | solution.py:14
  20.4 13.0 %collective-permute-start = (bf16[128,1152]{1,0:T(8,128)(2,1)S(1)}, bf16[128,1152]{1,0:T(8,128)(2,1)S(1)}, u32[]{:S(2)}, u32[]{:S(2)}) collective-permute-start(bf16[128,1152]{1,0:T(8,128)(2,1)S(1)} %copy.10), channel_id=1, source_target_pairs={{0,1},{1,2},{2,3},{3,4},{4,5},{5,6},{6,7},{7,8},{8,9},{9,10},{10,1... | collective-permute-start | bytes 884744 | tf_op jit(solution)/shard_map/while/body/eval_jaxpr/ppermute | solution.py:14
  22.0 14.7 %collective-permute-start.1 = (bf16[128,1152]{1,0:T(8,128)(2,1)S(1)}, bf16[128,1152]{1,0:T(8,128)(2,1)S(1)}, u32[]{:S(2)}, u32[]{:S(2)}) collective-permute-start(bf16[128,1152]{1,0:T(8,128)(2,1)S(1)} %copy.11), channel_id=1, source_target_pairs={{0,31},{1,0},{2,1},{3,2},{4,3},{5,4},{6,5},{7,6},{8,7},{9,8},{10,9... | collective-permute-start | bytes 884744 | tf_op jit(solution)/shard_map/while/body/eval_jaxpr/ppermute | solution.py:14
  36.8 13.0 %collective-permute-start = (bf16[128,1152]{1,0:T(8,128)(2,1)S(1)}, bf16[128,1152]{1,0:T(8,128)(2,1)S(1)}, u32[]{:S(2)}, u32[]{:S(2)}) collective-permute-start(bf16[128,1152]{1,0:T(8,128)(2,1)S(1)} %copy.10), channel_id=1, source_target_pairs={{0,1},{1,2},{2,3},{3,4},{4,5},{5,6},{6,7},{7,8},{8,9},{9,10},{10,1... | collective-permute-start | bytes 884744 | tf_op jit(solution)/shard_map/while/body/eval_jaxpr/ppermute | solution.py:14
  37.5 15.0 %collective-permute-start.1 = (bf16[128,1152]{1,0:T(8,128)(2,1)S(1)}, bf16[128,1152]{1,0:T(8,128)(2,1)S(1)}, u32[]{:S(2)}, u32[]{:S(2)}) collective-permute-start(bf16[128,1152]{1,0:T(8,128)(2,1)S(1)} %copy.11), channel_id=1, source_target_pairs={{0,31},{1,0},{2,1},{3,2},{4,3},{5,4},{6,5},{7,6},{8,7},{9,8},{10,9... | collective-permute-start | bytes 884744 | tf_op jit(solution)/shard_map/while/body/eval_jaxpr/ppermute | solution.py:14
  52.6 13.0 %collective-permute-start = (bf16[128,1152]{1,0:T(8,128)(2,1)S(1)}, bf16[128,1152]{1,0:T(8,128)(2,1)S(1)}, u32[]{:S(2)}, u32[]{:S(2)}) collective-permute-start(bf16[128,1152]{1,0:T(8,128)(2,1)S(1)} %copy.10), channel_id=1, source_target_pairs={{0,1},{1,2},{2,3},{3,4},{4,5},{5,6},{6,7},{7,8},{8,9},{9,10},{10,1... | collective-permute-start | bytes 884744 | tf_op jit(solution)/shard_map/while/body/eval_jaxpr/ppermute | solution.py:14
  53.7 15.1 %collective-permute-start.1 = (bf16[128,1152]{1,0:T(8,128)(2,1)S(1)}, bf16[128,1152]{1,0:T(8,128)(2,1)S(1)}, u32[]{:S(2)}, u32[]{:S(2)}) collective-permute-start(bf16[128,1152]{1,0:T(8,128)(2,1)S(1)} %copy.11), channel_id=1, source_target_pairs={{0,31},{1,0},{2,1},{3,2},{4,3},{5,4},{6,5},{7,6},{8,7},{9,8},{10,9... | collective-permute-start | bytes 884744 | tf_op jit(solution)/shard_map/while/body/eval_jaxpr/ppermute | solution.py:14
  68.9 12.9 %collective-permute-start = (bf16[128,1152]{1,0:T(8,128)(2,1)S(1)}, bf16[128,1152]{1,0:T(8,128)(2,1)S(1)}, u32[]{:S(2)}, u32[]{:S(2)}) collective-permute-start(bf16[128,1152]{1,0:T(8,128)(2,1)S(1)} %copy.10), channel_id=1, source_target_pairs={{0,1},{1,2},{2,3},{3,4},{4,5},{5,6},{6,7},{7,8},{8,9},{9,10},{10,1... | collective-permute-start | bytes 884744 | tf_op jit(solution)/shard_map/while/body/eval_jaxpr/ppermute | solution.py:14
  69.8 15.0 %collective-permute-start.1 = (bf16[128,1152]{1,0:T(8,128)(2,1)S(1)}, bf16[128,1152]{1,0:T(8,128)(2,1)S(1)}, u32[]{:S(2)}, u32[]{:S(2)}) collective-permute-start(bf16[128,1152]{1,0:T(8,128)(2,1)S(1)} %copy.11), channel_id=1, source_target_pairs={{0,31},{1,0},{2,1},{3,2},{4,3},{5,4},{6,5},{7,6},{8,7},{9,8},{10,9... | collective-permute-start | bytes 884744 | tf_op jit(solution)/shard_map/while/body/eval_jaxpr/ppermute | solution.py:14
  84.9 13.1 %collective-permute-start = (bf16[128,1152]{1,0:T(8,128)(2,1)S(1)}, bf16[128,1152]{1,0:T(8,128)(2,1)S(1)}, u32[]{:S(2)}, u32[]{:S(2)}) collective-permute-start(bf16[128,1152]{1,0:T(8,128)(2,1)S(1)} %copy.10), channel_id=1, source_target_pairs={{0,1},{1,2},{2,3},{3,4},{4,5},{5,6},{6,7},{7,8},{8,9},{9,10},{10,1... | collective-permute-start | bytes 884744 | tf_op jit(solution)/shard_map/while/body/eval_jaxpr/ppermute | solution.py:14
  86.3 14.4 %collective-permute-start.1 = (bf16[128,1152]{1,0:T(8,128)(2,1)S(1)}, bf16[128,1152]{1,0:T(8,128)(2,1)S(1)}, u32[]{:S(2)}, u32[]{:S(2)}) collective-permute-start(bf16[128,1152]{1,0:T(8,128)(2,1)S(1)} %copy.11), channel_id=1, source_target_pairs={{0,31},{1,0},{2,1},{3,2},{4,3},{5,4},{6,5},{7,6},{8,7},{9,8},{10,9... | collective-permute-start | bytes 884744 | tf_op jit(solution)/shard_map/while/body/eval_jaxpr/ppermute | solution.py:14
  100.7 12.9 %collective-permute-start = (bf16[128,1152]{1,0:T(8,128)(2,1)S(1)}, bf16[128,1152]{1,0:T(8,128)(2,1)S(1)}, u32[]{:S(2)}, u32[]{:S(2)}) collective-permute-start(bf16[128,1152]{1,0:T(8,128)(2,1)S(1)} %copy.10), channel_id=1, source_target_pairs={{0,1},{1,2},{2,3},{3,4},{4,5},{5,6},{6,7},{7,8},{8,9},{9,10},{10,1... | collective-permute-start | bytes 884744 | tf_op jit(solution)/shard_map/while/body/eval_jaxpr/ppermute | solution.py:14
  102.1 15.1 %collective-permute-start.1 = (bf16[128,1152]{1,0:T(8,128)(2,1)S(1)}, bf16[128,1152]{1,0:T(8,128)(2,1)S(1)}, u32[]{:S(2)}, u32[]{:S(2)}) collective-permute-start(bf16[128,1152]{1,0:T(8,128)(2,1)S(1)} %copy.11), channel_id=1, source_target_pairs={{0,31},{1,0},{2,1},{3,2},{4,3},{5,4},{6,5},{7,6},{8,7},{9,8},{10,9... | collective-permute-start | bytes 884744 | tf_op jit(solution)/shard_map/while/body/eval_jaxpr/ppermute | solution.py:14
  117.2 13.0 %collective-permute-start = (bf16[128,1152]{1,0:T(8,128)(2,1)S(1)}, bf16[128,1152]{1,0:T(8,128)(2,1)S(1)}, u32[]{:S(2)}, u32[]{:S(2)}) collective-permute-start(bf16[128,1152]{1,0:T(8,128)(2,1)S(1)} %copy.10), channel_id=1, source_target_pairs={{0,1},{1,2},{2,3},{3,4},{4,5},{5,6},{6,7},{7,8},{8,9},{9,10},{10,1... | collective-permute-start | bytes 884744 | tf_op jit(solution)/shard_map/while/body/eval_jaxpr/ppermute | solution.py:14
  118.2 14.9 %collective-permute-start.1 = (bf16[128,1152]{1,0:T(8,128)(2,1)S(1)}, bf16[128,1152]{1,0:T(8,128)(2,1)S(1)}, u32[]{:S(2)}, u32[]{:S(2)}) collective-permute-start(bf16[128,1152]{1,0:T(8,128)(2,1)S(1)} %copy.11), channel_id=1, source_target_pairs={{0,31},{1,0},{2,1},{3,2},{4,3},{5,4},{6,5},{7,6},{8,7},{9,8},{10,9... | collective-permute-start | bytes 884744 | tf_op jit(solution)/shard_map/while/body/eval_jaxpr/ppermute | solution.py:14
  133.2 13.0 %collective-permute-start = (bf16[128,1152]{1,0:T(8,128)(2,1)S(1)}, bf16[128,1152]{1,0:T(8,128)(2,1)S(1)}, u32[]{:S(2)}, u32[]{:S(2)}) collective-permute-start(bf16[128,1152]{1,0:T(8,128)(2,1)S(1)} %copy.10), channel_id=1, source_target_pairs={{0,1},{1,2},{2,3},{3,4},{4,5},{5,6},{6,7},{7,8},{8,9},{9,10},{10,1... | collective-permute-start | bytes 884744 | tf_op jit(solution)/shard_map/while/body/eval_jaxpr/ppermute | solution.py:14
  134.6 15.0 %collective-permute-start.1 = (bf16[128,1152]{1,0:T(8,128)(2,1)S(1)}, bf16[128,1152]{1,0:T(8,128)(2,1)S(1)}, u32[]{:S(2)}, u32[]{:S(2)}) collective-permute-start(bf16[128,1152]{1,0:T(8,128)(2,1)S(1)} %copy.11), channel_id=1, source_target_pairs={{0,31},{1,0},{2,1},{3,2},{4,3},{5,4},{6,5},{7,6},{8,7},{9,8},{10,9... | collective-permute-start | bytes 884744 | tf_op jit(solution)/shard_map/while/body/eval_jaxpr/ppermute | solution.py:14
  149.6 13.0 %collective-permute-start = (bf16[128,1152]{1,0:T(8,128)(2,1)S(1)}, bf16[128,1152]{1,0:T(8,128)(2,1)S(1)}, u32[]{:S(2)}, u32[]{:S(2)}) collective-permute-start(bf16[128,1152]{1,0:T(8,128)(2,1)S(1)} %copy.10), channel_id=1, source_target_pairs={{0,1},{1,2},{2,3},{3,4},{4,5},{5,6},{6,7},{7,8},{8,9},{9,10},{10,1... | collective-permute-start | bytes 884744 | tf_op jit(solution)/shard_map/while/body/eval_jaxpr/ppermute | solution.py:14
  150.3 15.1 %collective-permute-start.1 = (bf16[128,1152]{1,0:T(8,128)(2,1)S(1)}, bf16[128,1152]{1,0:T(8,128)(2,1)S(1)}, u32[]{:S(2)}, u32[]{:S(2)}) collective-permute-start(bf16[128,1152]{1,0:T(8,128)(2,1)S(1)} %copy.11), channel_id=1, source_target_pairs={{0,31},{1,0},{2,1},{3,2},{4,3},{5,4},{6,5},{7,6},{8,7},{9,8},{10,9... | collective-permute-start | bytes 884744 | tf_op jit(solution)/shard_map/while/body/eval_jaxpr/ppermute | solution.py:14
  165.4 13.0 %collective-permute-start = (bf16[128,1152]{1,0:T(8,128)(2,1)S(1)}, bf16[128,1152]{1,0:T(8,128)(2,1)S(1)}, u32[]{:S(2)}, u32[]{:S(2)}) collective-permute-start(bf16[128,1152]{1,0:T(8,128)(2,1)S(1)} %copy.10), channel_id=1, source_target_pairs={{0,1},{1,2},{2,3},{3,4},{4,5},{5,6},{6,7},{7,8},{8,9},{9,10},{10,1... | collective-permute-start | bytes 884744 | tf_op jit(solution)/shard_map/while/body/eval_jaxpr/ppermute | solution.py:14
  166.7 15.1 %collective-permute-start.1 = (bf16[128,1152]{1,0:T(8,128)(2,1)S(1)}, bf16[128,1152]{1,0:T(8,128)(2,1)S(1)}, u32[]{:S(2)}, u32[]{:S(2)}) collective-permute-start(bf16[128,1152]{1,0:T(8,128)(2,1)S(1)} %copy.11), channel_id=1, source_target_pairs={{0,31},{1,0},{2,1},{3,2},{4,3},{5,4},{6,5},{7,6},{8,7},{9,8},{10,9... | collective-permute-start | bytes 884744 | tf_op jit(solution)/shard_map/while/body/eval_jaxpr/ppermute | solution.py:14
  181.8 13.0 %collective-permute-start = (bf16[128,1152]{1,0:T(8,128)(2,1)S(1)}, bf16[128,1152]{1,0:T(8,128)(2,1)S(1)}, u32[]{:S(2)}, u32[]{:S(2)}) collective-permute-start(bf16[128,1152]{1,0:T(8,128)(2,1)S(1)} %copy.10), channel_id=1, source_target_pairs={{0,1},{1,2},{2,3},{3,4},{4,5},{5,6},{6,7},{7,8},{8,9},{9,10},{10,1... | collective-permute-start | bytes 884744 | tf_op jit(solution)/shard_map/while/body/eval_jaxpr/ppermute | solution.py:14
  182.8 15.0 %collective-permute-start.1 = (bf16[128,1152]{1,0:T(8,128)(2,1)S(1)}, bf16[128,1152]{1,0:T(8,128)(2,1)S(1)}, u32[]{:S(2)}, u32[]{:S(2)}) collective-permute-start(bf16[128,1152]{1,0:T(8,128)(2,1)S(1)} %copy.11), channel_id=1, source_target_pairs={{0,31},{1,0},{2,1},{3,2},{4,3},{5,4},{6,5},{7,6},{8,7},{9,8},{10,9... | collective-permute-start | bytes 884744 | tf_op jit(solution)/shard_map/while/body/eval_jaxpr/ppermute | solution.py:14
  197.8 13.0 %collective-permute-start = (bf16[128,1152]{1,0:T(8,128)(2,1)S(1)}, bf16[128,1152]{1,0:T(8,128)(2,1)S(1)}, u32[]{:S(2)}, u32[]{:S(2)}) collective-permute-start(bf16[128,1152]{1,0:T(8,128)(2,1)S(1)} %copy.10), channel_id=1, source_target_pairs={{0,1},{1,2},{2,3},{3,4},{4,5},{5,6},{6,7},{7,8},{8,9},{9,10},{10,1... | collective-permute-start | bytes 884744 | tf_op jit(solution)/shard_map/while/body/eval_jaxpr/ppermute | solution.py:14
  198.9 14.6 %collective-permute-start.1 = (bf16[128,1152]{1,0:T(8,128)(2,1)S(1)}, bf16[128,1152]{1,0:T(8,128)(2,1)S(1)}, u32[]{:S(2)}, u32[]{:S(2)}) collective-permute-start(bf16[128,1152]{1,0:T(8,128)(2,1)S(1)} %copy.11), channel_id=1, source_target_pairs={{0,31},{1,0},{2,1},{3,2},{4,3},{5,4},{6,5},{7,6},{8,7},{9,8},{10,9... | collective-permute-start | bytes 884744 | tf_op jit(solution)/shard_map/while/body/eval_jaxpr/ppermute | solution.py:14
  213.6 13.0 %collective-permute-start = (bf16[128,1152]{1,0:T(8,128)(2,1)S(1)}, bf16[128,1152]{1,0:T(8,128)(2,1)S(1)}, u32[]{:S(2)}, u32[]{:S(2)}) collective-permute-start(bf16[128,1152]{1,0:T(8,128)(2,1)S(1)} %copy.10), channel_id=1, source_target_pairs={{0,1},{1,2},{2,3},{3,4},{4,5},{5,6},{6,7},{7,8},{8,9},{9,10},{10,1... | collective-permute-start | bytes 884744 | tf_op jit(solution)/shard_map/while/body/eval_jaxpr/ppermute | solution.py:14
  215.0 15.1 %collective-permute-start.1 = (bf16[128,1152]{1,0:T(8,128)(2,1)S(1)}, bf16[128,1152]{1,0:T(8,128)(2,1)S(1)}, u32[]{:S(2)}, u32[]{:S(2)}) collective-permute-start(bf16[128,1152]{1,0:T(8,128)(2,1)S(1)} %copy.11), channel_id=1, source_target_pairs={{0,31},{1,0},{2,1},{3,2},{4,3},{5,4},{6,5},{7,6},{8,7},{9,8},{10,9... | collective-permute-start | bytes 884744 | tf_op jit(solution)/shard_map/while/body/eval_jaxpr/ppermute | solution.py:14
  230.1 13.0 %collective-permute-start = (bf16[128,1152]{1,0:T(8,128)(2,1)S(1)}, bf16[128,1152]{1,0:T(8,128)(2,1)S(1)}, u32[]{:S(2)}, u32[]{:S(2)}) collective-permute-start(bf16[128,1152]{1,0:T(8,128)(2,1)S(1)} %copy.10), channel_id=1, source_target_pairs={{0,1},{1,2},{2,3},{3,4},{4,5},{5,6},{6,7},{7,8},{8,9},{9,10},{10,1... | collective-permute-start | bytes 884744 | tf_op jit(solution)/shard_map/while/body/eval_jaxpr/ppermute | solution.py:14
  231.2 15.1 %collective-permute-start.1 = (bf16[128,1152]{1,0:T(8,128)(2,1)S(1)}, bf16[128,1152]{1,0:T(8,128)(2,1)S(1)}, u32[]{:S(2)}, u32[]{:S(2)}) collective-permute-start(bf16[128,1152]{1,0:T(8,128)(2,1)S(1)} %copy.11), channel_id=1, source_target_pairs={{0,31},{1,0},{2,1},{3,2},{4,3},{5,4},{6,5},{7,6},{8,7},{9,8},{10,9... | collective-permute-start | bytes 884744 | tf_op jit(solution)/shard_map/while/body/eval_jaxpr/ppermute | solution.py:14
where the time goes:
time: 250 us; the launch traced here: 249 us
  waiting for transfers between devices  121 us (48%)
  starting transfers between devices  82.9 us (33%)
  matrix products  21.2 us (8%)
  loops' own time  10.2 us (4%)
  local copies, waits for them, and re-layouts  9.49 us (4%)
  other arithmetic  3.38 us (1%)
    ppermute x30, waiting for transfers between devices, shifted(): return lax.ppermute(value, axis, pairs)  121 us
    ppermute x30, starting transfers between devices, shifted(): return lax.ppermute(value, axis, pairs)  82.9 us
    dot_general x16, matrix products, text_terms(): lax.dot_general(weights, image_block, (((0,), (0,)), ((), ())), preferred...  11.2 us
    another operation x1, loops' own time, per_device(): lax.scan(advance, (text_low, image_reduced, zeros, zeros), jnp.arange(win...  10.2 us
    dot_general x15, matrix products, advance(): jnp.dot(weights, text_block, preferred_element_type=jnp.float32)  9.34 us
    dynamic_slice x15, local copies, waits for them, and re-layouts, per_device(): lax.scan(advance, (text_low, image_reduced, zeros, zeros), jnp.arange(win...  8.73 us
  transfers between devices with their start and end apart: 30, of which 30 were waited for; matrix products, arithmetic and copies ran while one was open for 12% of the time, Pallas kernels for 0%

commit v1 on v0

v1 whole, which is shorter than its diff:
```python
import functools

import jax
import jax.numpy as jnp
from jax import lax
from jax.experimental import pallas as pl
from jax.experimental.pallas import tpu as pltpu
from jax.sharding import PartitionSpec as P

LOGIT_SCALE = 10.0
BIAS_LOGIT = -2.0
EPSILON = 1e-06
MESH = pl.DeviceIdType.MESH


def kernel(chips, depth, reach, window, image_ref, text_ref, image_out, text_out,
           held, total, own_scale, local_sem, send_sem, recv_sem):
    blk = lax.axis_index("blk")
    grp = lax.axis_index("grp")
    chip, core = blk // 2, blk % 2
    relayed = chips == 4 and reach == 2
    slots = 2 * (reach + 1)

    def view(kind):
        if kind == 0:
            return chip, core, grp
        return chips - 1 - chip, 1 - core, depth - 1 - grp

    def device(kind, c, k, z):
        c = (c + chips) % chips
        if kind == 0:
            return (2 * c + k, z)
        return (2 * (chips - 1 - c) + 1 - k, depth - 1 - z)

    def need(k, z, d, source_k, source_z):
        offset = (2 * d + k - source_k) * depth + z - source_z
        return (offset >= 0) & (offset < window)

    def chip_need(z, d, source_k, source_z):
        return need(0, z, d, source_k, source_z) | need(1, z, d, source_k, source_z)

    def arrives(kind, d, source_z):
        c, k, z = view(kind)
        wanted = chip_need(z, d, k, source_z)
        if relayed and d == 2:
            wanted = wanted | ((c % 2 == 1) & chip_need(z, 1, k, source_z))
        return wanted

    def copy(kind, path, source_slot, target_slot, z, target):
        return pltpu.make_async_remote_copy(
            src_ref=held.at[kind, source_slot, z],
            dst_ref=held.at[kind, target_slot, z],
            send_sem=send_sem.at[kind, path, z],
            recv_sem=recv_sem.at[kind, target_slot, z],
            device_id=target,
            device_id_type=MESH,
        )

    def own_sends(kind, z2):
        c, k, z = view(kind)
        sends = [
            ((z2 <= z) & (z + 1 < depth), 0, k, k, (c, k, z + 1)),
            ((z2 >= z) & (z >= 1), 1, k, k, (c, k, z - 1)),
        ]
        for d in range(1, reach + 1):
            wanted = chip_need(z, d, k, z2)
            if relayed and d == 1:
                wanted = wanted & (c % 2 == 0)
            if relayed and d == 2:
                wanted = wanted | ((c % 2 == 1) & chip_need(z, 1, k, z2))
            sends.append((wanted, 1 + d, k, 2 * d + k, (c + d, k, z)))
        sends.append((need(1 - k, z, 0, k, z2), 2 + reach, k, k, (c, 1 - k, z)))
        return sends

    def arrival_sends(kind, d, z2):
        c, k, z = view(kind)
        sends = []
        if relayed and d == 2:
            sends.append(((c % 2 == 1) & chip_need(z, 1, k, z2),
                          3 + reach, 4 + k, 2 + k, (c - 1, k, z)))
        sends.append((need(1 - k, z, d, k, z2), 3 + reach + d, 2 * d + k, 2 * d + k, (c, 1 - k, z)))
        return sends

    def each(kind, sends, z2, finish=False):
        for wanted, path, source_slot, target_slot, target in sends:
            @pl.when(wanted)
            def _():
                moved = copy(kind, path, source_slot, target_slot, z2, device(kind, *target))
                if finish:
                    moved.wait_send()
                else:
                    moved.start()

    def await_block(kind, slot, z2):
        c, k, z = view(kind)
        copy(kind, 0, slot, slot, z2, device(kind, c, 1 - k, z)).wait_recv()

    own = []
    for kind, ref in ((0, text_ref), (1, image_ref)):
        _, k, z = view(kind)
        loaded = pltpu.make_async_copy(ref, held.at[kind, k, z], local_sem.at[kind])
        loaded.start()
        own.append(loaded)

    barrier = pltpu.get_barrier_semaphore()

    def greet(target):
        pl.semaphore_signal(barrier, inc=1, device_id=target, device_id_type=MESH)

    greet((2 * chip + 1 - core, grp))
    if relayed:
        partners = [chip + 1 - 2 * (chip % 2), (chip + 2) % 4]
    else:
        partners = [(chip + d + chips) % chips for d in range(-reach, reach + 1) if d]
    for partner in partners:
        greet((2 * partner + core, grp))

    @pl.when(grp > 0)
    def _():
        greet((blk, grp - 1))

    @pl.when(grp < depth - 1)
    def _():
        greet((blk, grp + 1))

    for loaded in own:
        loaded.wait()
    pl.semaphore_wait(
        barrier,
        1 + len(partners) + (grp > 0).astype(jnp.int32) + (grp < depth - 1).astype(jnp.int32),
    )

    def views(kind):
        k = jnp.where(kind == 0, core, 1 - core)
        z = jnp.where(kind == 0, grp, depth - 1 - grp)
        return k, z

    def own_block(kind):
        k, z = views(kind)
        return held[kind, k, z]

    def inverse_length(block):
        wide = block.astype(jnp.float32)
        return lax.rsqrt(jnp.sum(wide * wide, axis=-1, keepdims=True) + EPSILON)

    rows = held.shape[3]

    def tile(kind, slot, z2):
        k, z = views(kind)
        other = held[kind, slot, z2]
        mine = own_block(1 - kind)
        columns = jnp.broadcast_to(inverse_length(other), (rows, rows)).T
        product = lax.dot_general(
            mine, other, (((1,), (1,)), ((), ())), preferred_element_type=jnp.float32
        )
        logits = LOGIT_SCALE * product * own_scale[kind] * columns + BIAS_LOGIT
        inverse = jnp.exp(-logits)
        weights = 1.0 / (1.0 + inverse)
        diagonal = lax.broadcasted_iota(jnp.int32, (rows, rows), 0) == lax.broadcasted_iota(
            jnp.int32, (rows, rows), 1
        )
        first = ((slot == k) & (z2 == z)).astype(jnp.float32)
        positive = jnp.where(diagonal, first, 0.0)
        weights = jnp.where(positive > 0.5, -inverse * weights, weights)
        scaled = (weights * columns).astype(jnp.bfloat16)
        total[kind] += jnp.dot(scaled, other, preferred_element_type=jnp.float32)

    def position(kind, sign, distance):
        _, _, z = view(kind)
        z2 = z + sign * distance
        valid = (z2 >= 0) & (z2 < depth) & (distance >= 0)
        if sign < 0:
            valid = valid & (distance > 0)
        return z2, valid

    def advance(turn, carry):
        for kind in (0, 1):
            for sign in (1, -1):
                z2, valid = position(kind, sign, turn)

                @pl.when(valid)
                def _():
                    @pl.when(turn > 0)
                    def _():
                        await_block(kind, view(kind)[1], z2)

                    each(kind, own_sends(kind, z2), z2)

        @pl.when(turn == 0)
        def _():
            def prepare(kind, carry):
                total[kind] = jnp.zeros(total.shape[1:], jnp.float32)
                own_scale[kind] = jnp.broadcast_to(inverse_length(own_block(1 - kind)), (rows, rows))
                return carry

            lax.fori_loop(0, 2, prepare, 0)

        for d in range(reach, 0, -1):
            for kind in (0, 1):
                for sign in (1, -1):
                    z2, valid = position(kind, sign, turn - 1)

                    @pl.when(valid & arrives(kind, d, z2))
                    def _():
                        await_block(kind, 2 * d + view(kind)[1], z2)
                        each(kind, arrival_sends(kind, d, z2), z2)

        def work(index, carry):
            slot = index // 4
            kind = (index // 2) % 2
            sign = 1 - 2 * (index % 2)
            k, z = views(kind)
            z2 = z + sign * (turn - 1)
            d, source_k = slot // 2, slot % 2
            valid = (turn > 0) & (z2 >= 0) & (z2 < depth) & ((sign > 0) | (turn > 1))

            @pl.when(valid & need(k, z, d, source_k, z2))
            def _():
                @pl.when(source_k != k)
                def _():
                    pltpu.make_async_remote_copy(
                        src_ref=held.at[kind, slot, z2],
                        dst_ref=held.at[kind, slot, z2],
                        send_sem=send_sem.at[kind, 0, z2],
                        recv_sem=recv_sem.at[kind, slot, z2],
                        device_id=(2 * chip + 1 - core, grp),
                        device_id_type=MESH,
                    ).wait_recv()

                tile(kind, slot, z2)

            return carry

        lax.fori_loop(0, 4 * slots, work, 0)
        return carry

    lax.fori_loop(0, depth + 1, advance, 0)

    for kind, out in ((0, image_out), (1, text_out)):
        scale = own_scale[kind][:, :1]
        unit = own_block(1 - kind).astype(jnp.float32) * scale
        grad = LOGIT_SCALE * total[kind]
        inner = jnp.sum(unit * grad, axis=-1, keepdims=True)
        out[...] = ((grad - unit * inner) * scale).astype(out.dtype)

    def settle(z2, carry):
        for kind in (0, 1):
            each(kind, own_sends(kind, z2), z2, finish=True)
            for d in range(1, reach + 1):
                @pl.when(arrives(kind, d, z2))
                def _():
                    each(kind, arrival_sends(kind, d, z2), z2, finish=True)
        return carry

    lax.fori_loop(0, depth, settle, 0)


def solution(mesh):
    cycle, depth = mesh.shape["blk"], mesh.shape["grp"]
    window = min(20, cycle * depth // 2)
    chips = cycle // 2
    reach = 1
    while (2 * reach + 1) * depth - (depth - 1) < window:
        reach += 1
    slots = 2 * (reach + 1)

    def per_device(image_embeds, text_embeds):
        rows, width = image_embeds.shape
        shape = jax.ShapeDtypeStruct((rows, width), jnp.bfloat16)
        return pl.pallas_call(
            functools.partial(kernel, chips, depth, reach, window),
            out_shape=(shape, shape),
            in_specs=[pl.BlockSpec(memory_space=pl.ANY)] * 2,
            out_specs=(pl.BlockSpec(memory_space=pltpu.VMEM),) * 2,
            scratch_shapes=[
                pltpu.VMEM((2, slots, depth, rows, width), jnp.bfloat16),
                pltpu.VMEM((2, rows, width), jnp.float32),
                pltpu.VMEM((2, rows, rows), jnp.float32),
                pltpu.SemaphoreType.DMA((2,)),
                pltpu.SemaphoreType.DMA((2, 4 + 2 * reach, depth)),
                pltpu.SemaphoreType.DMA((2, slots, depth)),
            ],
            compiler_params=pltpu.CompilerParams(collective_id=0, has_side_effects=True),
        )(image_embeds, text_embeds)

    placed = P(("blk", "grp"), None)
    return jax.shard_map(
        per_device, mesh=mesh, in_specs=(placed, placed), out_specs=(placed, placed), check_vma=False
    )
```

time: 250 us -> 92.8 us (0.37)
  the two profiles are of different devices: /device:TPU:0 before, /device:TPU:2 now
where the time goes in v1:
time: 92.8 us; the launch traced here: 92.7 us
  Pallas kernels  89.6 us (97%)
  local copies, waits for them, and re-layouts  2.46 us (3%)
    pallas_call x1, Pallas kernels, per_device(): pl.pallas_call(functools.partial(kernel, chips, depth, reach, window), ou...  89.6 us
    unnamed x4, local copies, waits for them, and re-layouts  2.46 us

profile of v1, /device:TPU:2, one launch (start us, length us, event | category | flops | bytes accessed | tf_op | source)
XLA Modules:
  0.0 92.7 jit_solution(16462970650984104766)
XLA Ops:
  0.6 89.6 %shard_map.41 = (bf16[128,1152]{1,0:T(8,128)(2,1)}, bf16[128,1152]{1,0:T(8,128)(2,1)}) custom-call(bf16[128,1152]{1,0:T(8,128)(2,1)} %image_ref.1, bf16[128,1152]{1,0:T(8,128)(2,1)} %text_ref.1), custom_call_target="tpu_custom_call" | custom-call | tf_op jit(solution)/shard_map/pallas_call | solution.py:270
  90.2 0.0 copy-start
  90.2 1.7 %copy.6 = bf16[128,1152]{1,0:T(8,128)(2,1)} copy(bf16[128,1152]{1,0:T(8,128)(2,1)} %get-tuple-element.4) | data formatting | bytes 589824
  92.0 0.0 copy-done
  92.0 0.7 copy.7
Async XLA Ops:
  90.2 1.8 %copy-start = (bf16[128,1152]{1,0:T(8,128)(2,1)S(1)}, bf16[128,1152]{1,0:T(8,128)(2,1)}, u32[]{:S(2)}) copy-start(bf16[128,1152]{1,0:T(8,128)(2,1)} %get-tuple-element.5) | copy-start | bytes 884740

commit v2 on v1

--- a/solution.py
+++ b/solution.py
@@ -18,19 +18,25 @@
     blk = lax.axis_index("blk")
     grp = lax.axis_index("grp")
     chip, core = blk // 2, blk % 2
-    relayed = chips == 4 and reach == 2
-    slots = 2 * (reach + 1)
+    relayed = chips == 4 and reach == 2 and 4 * depth - 1 < window
 
     def view(kind):
-        if kind == 0:
-            return chip, core, grp
-        return chips - 1 - chip, 1 - core, depth - 1 - grp
+        return (
+            chip + kind * (chips - 1 - 2 * chip),
+            core + kind * (1 - 2 * core),
+            grp + kind * (depth - 1 - 2 * grp),
+        )
 
     def device(kind, c, k, z):
         c = (c + chips) % chips
-        if kind == 0:
-            return (2 * c + k, z)
-        return (2 * (chips - 1 - c) + 1 - k, depth - 1 - z)
+        linear = 2 * c + k
+        return (
+            linear + kind * (2 * chips - 1 - 2 * linear),
+            z + kind * (depth - 1 - 2 * z),
+        )
+
+    first_kind = 1 - chip % 2 if relayed else 0
+    kinds = (first_kind, 1 - first_kind)
 
     def need(k, z, d, source_k, source_z):
         offset = (2 * d + k - source_k) * depth + z - source_z
@@ -42,8 +48,8 @@
     def arrives(kind, d, source_z):
         c, k, z = view(kind)
         wanted = chip_need(z, d, k, source_z)
-        if relayed and d == 2:
-            wanted = wanted | ((c % 2 == 1) & chip_need(z, 1, k, source_z))
+        if relayed:
+            wanted = wanted | ((d == 2) & (c % 2 == 1))
         return wanted
 
     def copy(kind, path, source_slot, target_slot, z, target):
@@ -65,9 +71,10 @@
         for d in range(1, reach + 1):
             wanted = chip_need(z, d, k, z2)
             if relayed and d == 1:
-                wanted = wanted & (c % 2 == 0)
+                inside = (z2 > 0) & (z2 < depth - 1)
+                wanted = (c % 2 == 0) & (inside | (z2 == z))
             if relayed and d == 2:
-                wanted = wanted | ((c % 2 == 1) & chip_need(z, 1, k, z2))
+                wanted = wanted | (c % 2 == 1)
             sends.append((wanted, 1 + d, k, 2 * d + k, (c + d, k, z)))
         sends.append((need(1 - k, z, 0, k, z2), 2 + reach, k, k, (c, 1 - k, z)))
         return sends
@@ -75,10 +82,15 @@
     def arrival_sends(kind, d, z2):
         c, k, z = view(kind)
         sends = []
-        if relayed and d == 2:
-            sends.append(((c % 2 == 1) & chip_need(z, 1, k, z2),
-                          3 + reach, 4 + k, 2 + k, (c - 1, k, z)))
-        sends.append((need(1 - k, z, d, k, z2), 3 + reach + d, 2 * d + k, 2 * d + k, (c, 1 - k, z)))
+        slot = 2 * d + k
+        if relayed:
+            sends.append(((c % 2 == 1) & (d == 2), 3 + reach, slot, 2 + k, (c - 1, k, z)))
+            outer = (c % 2 == 1) & (d == 1) & ((z2 == 0) | (z2 == depth - 1))
+            sends.append((outer & (z2 <= z) & (z + 1 < depth),
+                          4 + 2 * reach, slot, slot, (c, k, z + 1)))
+            sends.append((outer & (z2 >= z) & (z >= 1),
+                          5 + 2 * reach, slot, slot, (c, k, z - 1)))
+        sends.append((need(1 - k, z, d, k, z2), 3 + reach + d, slot, slot, (c, 1 - k, z)))
         return sends
 
     def each(kind, sends, z2, finish=False):
@@ -130,13 +142,8 @@
         1 + len(partners) + (grp > 0).astype(jnp.int32) + (grp < depth - 1).astype(jnp.int32),
     )
 
-    def views(kind):
-        k = jnp.where(kind == 0, core, 1 - core)
-        z = jnp.where(kind == 0, grp, depth - 1 - grp)
-        return k, z
-
     def own_block(kind):
-        k, z = views(kind)
+        _, k, z = view(kind)
         return held[kind, k, z]
 
     def inverse_length(block):
@@ -146,7 +153,7 @@
     rows = held.shape[3]
 
     def tile(kind, slot, z2):
-        k, z = views(kind)
+        _, k, z = view(kind)
         other = held[kind, slot, z2]
         mine = own_block(1 - kind)
         columns = jnp.broadcast_to(inverse_length(other), (rows, rows)).T
@@ -169,12 +176,10 @@
         _, _, z = view(kind)
         z2 = z + sign * distance
         valid = (z2 >= 0) & (z2 < depth) & (distance >= 0)
-        if sign < 0:
-            valid = valid & (distance > 0)
-        return z2, valid
+        return z2, valid & ((sign > 0) | (distance > 0))
 
     def advance(turn, carry):
-        for kind in (0, 1):
+        for kind in kinds:
             for sign in (1, -1):
                 z2, valid = position(kind, sign, turn)
 
@@ -195,44 +200,38 @@
 
             lax.fori_loop(0, 2, prepare, 0)
 
-        for d in range(reach, 0, -1):
-            for kind in (0, 1):
+        def stage(step, carry):
+            d = jnp.where(step == 0, reach, jnp.where(step == 1, 0, reach - step + 1))
+            distance = turn - (d > 0).astype(jnp.int32)
+            for kind in kinds:
                 for sign in (1, -1):
-                    z2, valid = position(kind, sign, turn - 1)
-
-                    @pl.when(valid & arrives(kind, d, z2))
+                    z2, valid = position(kind, sign, distance)
+
+                    @pl.when((d > 0) & valid & arrives(kind, d, z2))
                     def _():
                         await_block(kind, 2 * d + view(kind)[1], z2)
                         each(kind, arrival_sends(kind, d, z2), z2)
 
-        def work(index, carry):
-            slot = index // 4
-            kind = (index // 2) % 2
-            sign = 1 - 2 * (index % 2)
-            k, z = views(kind)
-            z2 = z + sign * (turn - 1)
-            d, source_k = slot // 2, slot % 2
-            valid = (turn > 0) & (z2 >= 0) & (z2 < depth) & ((sign > 0) | (turn > 1))
-
-            @pl.when(valid & need(k, z, d, source_k, z2))
-            def _():
-                @pl.when(source_k != k)
+            def work(index, carry):
+                kind = first_kind + ((index // 2) % 2) * (1 - 2 * first_kind)
+                _, k, z = view(kind)
+                source_k = (k + index // 4) % 2
+                z2, valid = position(kind, 1 - 2 * (index % 2), distance)
+                slot = 2 * d + source_k
+
+                @pl.when(valid & need(k, z, d, source_k, z2))
                 def _():
-                    pltpu.make_async_remote_copy(
-                        src_ref=held.at[kind, slot, z2],
-                        dst_ref=held.at[kind, slot, z2],
-                        send_sem=send_sem.at[kind, 0, z2],
-                        recv_sem=recv_sem.at[kind, slot, z2],
-                        device_id=(2 * chip + 1 - core, grp),
-                        device_id_type=MESH,
-                    ).wait_recv()
-
-                tile(kind, slot, z2)
-
-            return carry
-
-        lax.fori_loop(0, 4 * slots, work, 0)
-        return carry
+                    @pl.when(source_k != k)
+                    def _():
+                        await_block(kind, slot, z2)
+
+                    tile(kind, slot, z2)
+
+                return carry
+
+            return lax.fori_loop(0, 8, work, carry)
+
+        return lax.fori_loop(0, reach + 1, stage, carry)
 
     lax.fori_loop(0, depth + 1, advance, 0)
 
@@ -277,7 +276,7 @@
                 pltpu.VMEM((2, rows, width), jnp.float32),
                 pltpu.VMEM((2, rows, rows), jnp.float32),
                 pltpu.SemaphoreType.DMA((2,)),
-                pltpu.SemaphoreType.DMA((2, 4 + 2 * reach, depth)),
+                pltpu.SemaphoreType.DMA((2, 6 + 2 * reach, depth)),
                 pltpu.SemaphoreType.DMA((2, slots, depth)),
             ],
             compiler_params=pltpu.CompilerParams(collective_id=0, has_side_effects=True),

time: 92.8 us -> 77.5 us (0.84)
  the two profiles are of different devices: /device:TPU:2 before, /device:TPU:0 now
where the time goes in v2:
time: 77.5 us; the launch traced here: 77.4 us
  Pallas kernels  74.3 us (96%)
  local copies, waits for them, and re-layouts  2.46 us (3%)
    pallas_call x1, Pallas kernels, per_device(): pl.pallas_call(functools.partial(kernel, chips, depth, reach, window), ou...  74.3 us
    unnamed x4, local copies, waits for them, and re-layouts  2.46 us

profile of v2, /device:TPU:0, one launch (start us, length us, event | category | flops | bytes accessed | tf_op | source)
XLA Modules:
  0.0 77.4 jit_solution(10116770385465856093)
XLA Ops:
  0.6 74.3 %shard_map.41 = (bf16[128,1152]{1,0:T(8,128)(2,1)}, bf16[128,1152]{1,0:T(8,128)(2,1)}) custom-call(bf16[128,1152]{1,0:T(8,128)(2,1)} %image_ref.1, bf16[128,1152]{1,0:T(8,128)(2,1)} %text_ref.1), custom_call_target="tpu_custom_call" | custom-call | tf_op jit(solution)/shard_map/pallas_call | solution.py:269
  74.9 0.0 copy-start
  74.9 1.7 %copy.6 = bf16[128,1152]{1,0:T(8,128)(2,1)} copy(bf16[128,1152]{1,0:T(8,128)(2,1)} %get-tuple-element.4) | data formatting | bytes 589824
  76.7 0.0 copy-done
  76.7 0.7 copy.7
Async XLA Ops:
  74.9 1.8 %copy-start = (bf16[128,1152]{1,0:T(8,128)(2,1)S(1)}, bf16[128,1152]{1,0:T(8,128)(2,1)}, u32[]{:S(2)}) copy-start(bf16[128,1152]{1,0:T(8,128)(2,1)} %get-tuple-element.5) | copy-start | bytes 884740

commit v3 on v2

--- a/solution.py
+++ b/solution.py
@@ -178,45 +178,46 @@
         valid = (z2 >= 0) & (z2 < depth) & (distance >= 0)
         return z2, valid & ((sign > 0) | (distance > 0))
 
-    def advance(turn, carry):
-        for kind in kinds:
-            for sign in (1, -1):
-                z2, valid = position(kind, sign, turn)
-
-                @pl.when(valid)
-                def _():
-                    @pl.when(turn > 0)
-                    def _():
-                        await_block(kind, view(kind)[1], z2)
-
-                    each(kind, own_sends(kind, z2), z2)
-
-        @pl.when(turn == 0)
-        def _():
-            def prepare(kind, carry):
-                total[kind] = jnp.zeros(total.shape[1:], jnp.float32)
-                own_scale[kind] = jnp.broadcast_to(inverse_length(own_block(1 - kind)), (rows, rows))
-                return carry
-
-            lax.fori_loop(0, 2, prepare, 0)
+    def prepare(kind, carry):
+        total[kind] = jnp.zeros(total.shape[1:], jnp.float32)
+        own_scale[kind] = jnp.broadcast_to(inverse_length(own_block(1 - kind)), (rows, rows))
+        return carry
+
+    def start_own(kind):
+        _, _, z = view(kind)
+        each(kind, own_sends(kind, z), z)
+
+    for kind in kinds:
+        start_own(kind)
+    lax.fori_loop(0, 2, prepare, 0)
+
+    def half_turn(index, carry):
+        turn = index // 2
+        kind = first_kind + (index % 2) * (1 - 2 * first_kind)
+        _, k, z = view(kind)
+
+        for sign in (1, -1):
+            z2, valid = position(kind, sign, turn)
+
+            @pl.when(valid & (turn > 0))
+            def _():
+                await_block(kind, k, z2)
+                each(kind, own_sends(kind, z2), z2)
 
         def stage(step, carry):
             d = jnp.where(step == 0, reach, jnp.where(step == 1, 0, reach - step + 1))
             distance = turn - (d > 0).astype(jnp.int32)
-            for kind in kinds:
-                for sign in (1, -1):
-                    z2, valid = position(kind, sign, distance)
-
-                    @pl.when((d > 0) & valid & arrives(kind, d, z2))
-                    def _():
-                        await_block(kind, 2 * d + view(kind)[1], z2)
-                        each(kind, arrival_sends(kind, d, z2), z2)
-
-            def work(index, carry):
-                kind = first_kind + ((index // 2) % 2) * (1 - 2 * first_kind)
-                _, k, z = view(kind)
-                source_k = (k + index // 4) % 2
-                z2, valid = position(kind, 1 - 2 * (index % 2), distance)
+            for sign in (1, -1):
+                z2, valid = position(kind, sign, distance)
+
+                @pl.when((d > 0) & valid & arrives(kind, d, z2))
+                def _():
+                    await_block(kind, 2 * d + k, z2)
+                    each(kind, arrival_sends(kind, d, z2), z2)
+
+            def work(item, carry):
+                source_k = (k + item // 2) % 2
+                z2, valid = position(kind, 1 - 2 * (item % 2), distance)
                 slot = 2 * d + source_k
 
                 @pl.when(valid & need(k, z, d, source_k, z2))
@@ -229,11 +230,11 @@
 
                 return carry
 
-            return lax.fori_loop(0, 8, work, carry)
+            return lax.fori_loop(0, 4, work, carry)
 
         return lax.fori_loop(0, reach + 1, stage, carry)
 
-    lax.fori_loop(0, depth + 1, advance, 0)
+    lax.fori_loop(0, 2 * (depth + 1), half_turn, 0)
 
     for kind, out in ((0, image_out), (1, text_out)):
         scale = own_scale[kind][:, :1]

time: 77.5 us -> 65.2 us (0.84)
  Pallas kernels: 74.3 us -> 61.5 us
    pallas_call x1, Pallas kernels: 74.3 us -> 61.5 us  [per_device(): pl.pallas_call(functools.partial(kernel, chips, depth, reach, window), ou...]
where the time goes in v3:
time: 65.2 us; the launch traced here: 64.6 us
  Pallas kernels  61.5 us (94%)
  local copies, waits for them, and re-layouts  2.46 us (4%)
    pallas_call x1, Pallas kernels, per_device(): pl.pallas_call(functools.partial(kernel, chips, depth, reach, window), ou...  61.5 us
    unnamed x4, local copies, waits for them, and re-layouts  2.46 us

profile of v3, /device:TPU:0, one launch (start us, length us, event | category | flops | bytes accessed | tf_op | source)
XLA Modules:
  0.0 64.6 jit_solution(9079607048903881504)
XLA Ops:
  0.6 61.5 %shard_map.41 = (bf16[128,1152]{1,0:T(8,128)(2,1)}, bf16[128,1152]{1,0:T(8,128)(2,1)}) custom-call(bf16[128,1152]{1,0:T(8,128)(2,1)} %image_ref.1, bf16[128,1152]{1,0:T(8,128)(2,1)} %text_ref.1), custom_call_target="tpu_custom_call" | custom-call | tf_op jit(solution)/shard_map/pallas_call | solution.py:270
  62.1 0.0 copy-start
  62.1 1.7 %copy.6 = bf16[128,1152]{1,0:T(8,128)(2,1)} copy(bf16[128,1152]{1,0:T(8,128)(2,1)} %get-tuple-element.4) | data formatting | bytes 589824
  63.9 0.0 copy-done
  63.9 0.7 %copy.7 = bf16[128,1152]{1,0:T(8,128)(2,1)} copy(bf16[128,1152]{1,0:T(8,128)(2,1)S(1)} %copy-done) | data formatting | bytes 589824
Async XLA Ops:
  62.1 1.8 %copy-start = (bf16[128,1152]{1,0:T(8,128)(2,1)S(1)}, bf16[128,1152]{1,0:T(8,128)(2,1)}, u32[]{:S(2)}) copy-start(bf16[128,1152]{1,0:T(8,128)(2,1)} %get-tuple-element.5) | copy-start | bytes 884740

commit v4 on v3

--- a/solution.py
+++ b/solution.py
@@ -71,8 +71,7 @@
         for d in range(1, reach + 1):
             wanted = chip_need(z, d, k, z2)
             if relayed and d == 1:
-                inside = (z2 > 0) & (z2 < depth - 1)
-                wanted = (c % 2 == 0) & (inside | (z2 == z))
+                wanted = c % 2 == 0
             if relayed and d == 2:
                 wanted = wanted | (c % 2 == 1)
             sends.append((wanted, 1 + d, k, 2 * d + k, (c + d, k, z)))
@@ -84,8 +83,11 @@
         sends = []
         slot = 2 * d + k
         if relayed:
-            sends.append(((c % 2 == 1) & (d == 2), 3 + reach, slot, 2 + k, (c - 1, k, z)))
-            outer = (c % 2 == 1) & (d == 1) & ((z2 == 0) | (z2 == depth - 1))
+            outer = (z2 == 0) | (z2 == depth - 1)
+            crossing = (z2 == z) | jnp.logical_not(outer)
+            sends.append(((c % 2 == 1) & (d == 2) & crossing,
+                          3 + reach, slot, 2 + k, (c - 1, k, z)))
+            outer = (c % 2 == 0) & (d == 1) & outer
             sends.append((outer & (z2 <= z) & (z + 1 < depth),
                           4 + 2 * reach, slot, slot, (c, k, z + 1)))
             sends.append((outer & (z2 >= z) & (z >= 1),
@@ -191,50 +193,60 @@
         start_own(kind)
     lax.fori_loop(0, 2, prepare, 0)
 
-    def half_turn(index, carry):
-        turn = index // 2
-        kind = first_kind + (index % 2) * (1 - 2 * first_kind)
+    steps = reach + 1
+
+    def advance(index, carry):
+        turn, part = index // (2 * steps), index % (2 * steps)
+        which, step = part // steps, part % steps
+        d = jnp.where(step == 0, reach, jnp.where(step == 1, 0, reach - step + 1))
+        opens = step == 0
+        receives = d > 0
+        computes = index >= 0
+        if relayed:
+            last = turn == depth
+            far = (part == 0) | (part == 3) | (part == 5)
+            which = jnp.where(last, part % 2, which)
+            d = jnp.where(last, jnp.where(far, 2, 1), d)
+            receives = jnp.where(last, part < 4, receives)
+            computes = jnp.logical_not(last & ((part == 2) | (part == 3)))
+        kind = first_kind + which * (1 - 2 * first_kind)
         _, k, z = view(kind)
+        distance = turn - (d > 0).astype(jnp.int32)
 
         for sign in (1, -1):
             z2, valid = position(kind, sign, turn)
 
-            @pl.when(valid & (turn > 0))
+            @pl.when(valid & opens & (turn > 0))
             def _():
                 await_block(kind, k, z2)
                 each(kind, own_sends(kind, z2), z2)
 
-        def stage(step, carry):
-            d = jnp.where(step == 0, reach, jnp.where(step == 1, 0, reach - step + 1))
-            distance = turn - (d > 0).astype(jnp.int32)
-            for sign in (1, -1):
-                z2, valid = position(kind, sign, distance)
-
-                @pl.when((d > 0) & valid & arrives(kind, d, z2))
+        for sign in (1, -1):
+            z2, valid = position(kind, sign, distance)
+
+            @pl.when(receives & valid & arrives(kind, d, z2))
+            def _():
+                await_block(kind, 2 * d + k, z2)
+                each(kind, arrival_sends(kind, d, z2), z2)
+
+        def work(item, carry):
+            source_k = (k + item // 2) % 2
+            z2, valid = position(kind, 1 - 2 * (item % 2), distance)
+            slot = 2 * d + source_k
+
+            @pl.when(valid & computes & need(k, z, d, source_k, z2))
+            def _():
+                @pl.when(source_k != k)
                 def _():
-                    await_block(kind, 2 * d + k, z2)
-                    each(kind, arrival_sends(kind, d, z2), z2)
-
-            def work(item, carry):
-                source_k = (k + item // 2) % 2
-                z2, valid = position(kind, 1 - 2 * (item % 2), distance)
-                slot = 2 * d + source_k
-
-                @pl.when(valid & need(k, z, d, source_k, z2))
-                def _():
-                    @pl.when(source_k != k)
-                    def _():
-                        await_block(kind, slot, z2)
-
-                    tile(kind, slot, z2)
-
-                return carry
-
-            return lax.fori_loop(0, 4, work, carry)
-
-        return lax.fori_loop(0, reach + 1, stage, carry)
-
-    lax.fori_loop(0, 2 * (depth + 1), half_turn, 0)
+                    await_block(kind, slot, z2)
+
+                tile(kind, slot, z2)
+
+            return carry
+
+        return lax.fori_loop(0, 4, work, carry)
+
+    lax.fori_loop(0, 2 * steps * (depth + 1), advance, 0)
 
     for kind, out in ((0, image_out), (1, text_out)):
         scale = own_scale[kind][:, :1]

time: 65.2 us -> 70.6 us (1.083)
  Pallas kernels: 61.5 us -> 67.2 us
    pallas_call x1, Pallas kernels: 61.5 us -> 67.2 us  [per_device(): pl.pallas_call(functools.partial(kernel, chips, depth, reach, window), ou...]
where the time goes in v4:
time: 70.6 us; the launch traced here: 70.3 us
  Pallas kernels  67.2 us (95%)
  local copies, waits for them, and re-layouts  2.46 us (3%)
    pallas_call x1, Pallas kernels, per_device(): pl.pallas_call(functools.partial(kernel, chips, depth, reach, window), ou...  67.2 us
    unnamed x4, local copies, waits for them, and re-layouts  2.46 us

profile of v4, /device:TPU:0, one launch (start us, length us, event | category | flops | bytes accessed | tf_op | source)
XLA Modules:
  0.0 70.3 jit_solution(17415698278128650919)
XLA Ops:
  0.6 67.2 %shard_map.41 = (bf16[128,1152]{1,0:T(8,128)(2,1)}, bf16[128,1152]{1,0:T(8,128)(2,1)}) custom-call(bf16[128,1152]{1,0:T(8,128)(2,1)} %image_ref.1, bf16[128,1152]{1,0:T(8,128)(2,1)} %text_ref.1), custom_call_target="tpu_custom_call" | custom-call | tf_op jit(solution)/shard_map/pallas_call | solution.py:282
  67.8 0.0 copy-start
  67.8 1.7 %copy.6 = bf16[128,1152]{1,0:T(8,128)(2,1)} copy(bf16[128,1152]{1,0:T(8,128)(2,1)} %get-tuple-element.4) | data formatting | bytes 589824
  69.5 0.0 copy-done
  69.5 0.7 %copy.7 = bf16[128,1152]{1,0:T(8,128)(2,1)} copy(bf16[128,1152]{1,0:T(8,128)(2,1)S(1)} %copy-done) | data formatting | bytes 589824
Async XLA Ops:
  67.8 1.8 %copy-start = (bf16[128,1152]{1,0:T(8,128)(2,1)S(1)}, bf16[128,1152]{1,0:T(8,128)(2,1)}, u32[]{:S(2)}) copy-start(bf16[128,1152]{1,0:T(8,128)(2,1)} %get-tuple-element.5) | copy-start | bytes 884740

commit v5 on v4

--- a/solution.py
+++ b/solution.py
@@ -71,7 +71,8 @@
         for d in range(1, reach + 1):
             wanted = chip_need(z, d, k, z2)
             if relayed and d == 1:
-                wanted = c % 2 == 0
+                inside = (z2 > 0) & (z2 < depth - 1)
+                wanted = (c % 2 == 0) & (inside | (z2 == z))
             if relayed and d == 2:
                 wanted = wanted | (c % 2 == 1)
             sends.append((wanted, 1 + d, k, 2 * d + k, (c + d, k, z)))
@@ -83,11 +84,8 @@
         sends = []
         slot = 2 * d + k
         if relayed:
-            outer = (z2 == 0) | (z2 == depth - 1)
-            crossing = (z2 == z) | jnp.logical_not(outer)
-            sends.append(((c % 2 == 1) & (d == 2) & crossing,
-                          3 + reach, slot, 2 + k, (c - 1, k, z)))
-            outer = (c % 2 == 0) & (d == 1) & outer
+            sends.append(((c % 2 == 1) & (d == 2), 3 + reach, slot, 2 + k, (c - 1, k, z)))
+            outer = (c % 2 == 1) & (d == 1) & ((z2 == 0) | (z2 == depth - 1))
             sends.append((outer & (z2 <= z) & (z + 1 < depth),
                           4 + 2 * reach, slot, slot, (c, k, z + 1)))
             sends.append((outer & (z2 >= z) & (z >= 1),
@@ -204,11 +202,11 @@
         computes = index >= 0
         if relayed:
             last = turn == depth
-            far = (part == 0) | (part == 3) | (part == 5)
-            which = jnp.where(last, part % 2, which)
+            far = (part == 0) | (part == 2) | (part == 4)
+            which = jnp.where(last, ((part == 2) | (part >= 4)).astype(jnp.int32), which)
             d = jnp.where(last, jnp.where(far, 2, 1), d)
-            receives = jnp.where(last, part < 4, receives)
-            computes = jnp.logical_not(last & ((part == 2) | (part == 3)))
+            receives = jnp.where(last, (part < 3) | (part == 5), receives)
+            computes = jnp.logical_not(last & ((part == 1) | (part == 2)))
         kind = first_kind + which * (1 - 2 * first_kind)
         _, k, z = view(kind)
         distance = turn - (d > 0).astype(jnp.int32)

time: 70.6 us -> 65.3 us (0.925)
  Pallas kernels: 67.2 us -> 61.6 us
    pallas_call x1, Pallas kernels: 67.2 us -> 61.6 us  [per_device(): pl.pallas_call(functools.partial(kernel, chips, depth, reach, window), ou...]
where the time goes in v5:
time: 65.3 us; the launch traced here: 64.7 us
  Pallas kernels  61.6 us (94%)
  local copies, waits for them, and re-layouts  2.46 us (4%)
    pallas_call x1, Pallas kernels, per_device(): pl.pallas_call(functools.partial(kernel, chips, depth, reach, window), ou...  61.6 us
    unnamed x4, local copies, waits for them, and re-layouts  2.46 us

profile of v5, /device:TPU:0, one launch (start us, length us, event | category | flops | bytes accessed | tf_op | source)
XLA Modules:
  0.0 64.7 jit_solution(10522206346795320764)
XLA Ops:
  0.6 61.6 %shard_map.41 = (bf16[128,1152]{1,0:T(8,128)(2,1)}, bf16[128,1152]{1,0:T(8,128)(2,1)}) custom-call(bf16[128,1152]{1,0:T(8,128)(2,1)} %image_ref.1, bf16[128,1152]{1,0:T(8,128)(2,1)} %text_ref.1), custom_call_target="tpu_custom_call" | custom-call | tf_op jit(solution)/shard_map/pallas_call | solution.py:280
  62.2 0.0 copy-start
  62.2 1.7 %copy.6 = bf16[128,1152]{1,0:T(8,128)(2,1)} copy(bf16[128,1152]{1,0:T(8,128)(2,1)} %get-tuple-element.4) | data formatting | bytes 589824
  64.0 0.0 copy-done
  64.0 0.7 %copy.7 = bf16[128,1152]{1,0:T(8,128)(2,1)} copy(bf16[128,1152]{1,0:T(8,128)(2,1)S(1)} %copy-done) | data formatting | bytes 589824
Async XLA Ops:
  62.2 1.8 %copy-start = (bf16[128,1152]{1,0:T(8,128)(2,1)S(1)}, bf16[128,1152]{1,0:T(8,128)(2,1)}, u32[]{:S(2)}) copy-start(bf16[128,1152]{1,0:T(8,128)(2,1)} %get-tuple-element.5) | copy-start | bytes 884740
